TPU v7x, 256 devices: a 4x2x16 block of a 4x16x16 slice. The times are simulated.
256 devices in a mesh: grp: 2 (over y), row: 32 (over z, core), col: 4 (over x).
Axes of the slice: x: 4, y: 2, z: 16, core: 2. Of those that a mesh axis runs over, the one named last changes fastest.
The devices are a block of a 4x16x16 slice.
Arguments:
- pair: bfloat16 [768, 384, 128], P(('grp', 'row'), 'col'), parts along dimension 0, may hold values from -6 to 6
- token_count: int32 [2], P('grp'), parts along dimension 0, may hold values from 288 to 384
- tri_in: bfloat16 [2, 128, 512], replicated, may hold values from -0.5 to 0.5
- tri_gate: bfloat16 [2, 128, 128], replicated, may hold values from -0.5 to 0.5
- tri_out: bfloat16 [2, 128, 128], replicated, may hold values from -0.5 to 0.5
- trans_in: bfloat16 [128, 1024], replicated, may hold values from -0.5 to 0.5
- trans_out: bfloat16 [512, 128], replicated, may hold values from -0.25 to 0.25
Outputs:
- pair_out: bfloat16 [768, 384, 128], P(('grp', 'row'), 'col'), parts along dimension 0
There are 2 independent parts, one for each index of `grp`. A program takes and returns all parts, laid end to end along the dimension named above; an argument that names none is the same for every part. Nothing has to cross between parts.
Inputs may be any that keep to these rules, and one draw needn't show every extreme that they name: `token_count`: the number of real tokens of the complex; pair entries with either token index at or past it are padding.
All inputs are finite; a program needn't handle non-finite values.
Results may differ from a plain program's by a relative error of at most 0.015.
Values may be sent and summed in bfloat16 or wider, within the bound.
A program may use at most 64 MiB of HBM per device.

v0:
```python
import jax
import jax.numpy as jnp
from jax import lax
from jax.sharding import Mesh
from jax.sharding import PartitionSpec as P

ROW = ("row_0", "row_1")
GRP_ROW = ("grp", "row_0", "row_1")


def split_up(value, dim, size):
    lengths = value.shape
    blocks = value.reshape(*lengths[:dim], size, lengths[dim] // size, *lengths[dim + 1 :])
    return jnp.moveaxis(blocks, dim, 0)


def sum_at_owner(value, axis, dim):
    blocks = split_up(value, dim, lax.axis_size(axis))
    arrived = lax.all_to_all(blocks, axis, split_axis=0, concat_axis=0, tiled=True)
    return arrived.sum(axis=0)


def sent_to_all(value, axis):
    copies = jnp.broadcast_to(value, (lax.axis_size(axis), *value.shape))
    return lax.all_to_all(copies, axis, split_axis=0, concat_axis=0, tiled=True)


def laid_out(blocks, dim):
    lengths = list(blocks.shape[1:])
    lengths[dim] *= blocks.shape[0]
    return jnp.moveaxis(blocks, 0, dim).reshape(lengths)


def gather_directly(value, axis, dim):
    blocks = sent_to_all(value, axis)
    return laid_out(blocks, dim)


def exchange_in_order(blocks, axes, sequence):
    lengths = [lax.axis_size(a) for a in axes]
    blocks = blocks.reshape(*lengths, *blocks.shape[1:])
    for k in sequence:
        blocks = lax.all_to_all(blocks, axes[k], split_axis=k, concat_axis=k, tiled=True)
    return blocks.reshape(-1, *blocks.shape[len(axes) :])


def two_step_exchange(value, groups, sequence, split_dim, concat_dim):
    size = lax.axis_size(groups[0]) * lax.axis_size(groups[1])
    blocks = split_up(value, split_dim, size)
    return laid_out(exchange_in_order(blocks, groups, sequence), concat_dim)


def layer_norm(values, along):
    average = jnp.mean(values, axis=along, keepdims=True)
    centred = values - average
    spread = jnp.mean(centred * centred, axis=along, keepdims=True)
    return centred * lax.rsqrt(spread + 1e-05)


def contract_rows(left_side, right_side):
    return jnp.einsum("hik,hjk->hij", left_side, right_side, preferred_element_type=jnp.float32)


def contract_columns(left_side, right_side):
    return jnp.einsum("hki,hkj->hij", left_side, right_side, preferred_element_type=jnp.float32)


def body(pair, token_count, tri_in, tri_gate, tri_out, trans_in, trans_out):
    tile_rows, tile_cols, pair_width = pair.shape
    hidden = tri_out.shape[1]
    ffn_width = trans_out.shape[0]
    row_place = lax.axis_index(ROW)
    col_place = lax.axis_index("col")
    row_first = row_place * tile_rows
    col_first = col_place * tile_cols
    token_limit = token_count[0]
    row_keep = (row_first + jnp.arange(tile_rows, dtype=jnp.int32) < token_limit).astype(
        jnp.float32
    )
    col_keep = (col_first + jnp.arange(tile_cols, dtype=jnp.int32) < token_limit).astype(
        jnp.float32
    )
    keep_mask = row_keep[:, None] * col_keep[None, :]

    def project(stream, which_side):
        normed = layer_norm(stream.astype(jnp.float32), 2).astype(jnp.bfloat16)
        weight = tri_in[which_side].reshape(pair_width, 4, hidden)
        projected = jnp.einsum("ijc,cgh->ghij", normed, weight, preferred_element_type=jnp.float32)
        left_side = (keep_mask * jax.nn.sigmoid(projected[2]) * projected[0]).astype(jnp.bfloat16)
        right_side = (keep_mask * jax.nn.sigmoid(projected[3]) * projected[1]).astype(jnp.bfloat16)
        gate_value = jax.nn.sigmoid(
            jnp.dot(normed, tri_gate[which_side], preferred_element_type=jnp.float32)
        )
        return (left_side, right_side, gate_value)

    def finish(stream, mixed_sum, gate_value, which_side):
        normed = layer_norm(mixed_sum, 0).astype(jnp.bfloat16)
        update = gate_value * jnp.einsum(
            "hij,hc->ijc", normed, tri_out[which_side], preferred_element_type=jnp.float32
        )
        return (stream.astype(jnp.float32) + keep_mask[:, :, None] * update).astype(jnp.bfloat16)

    left_side, right_side, gate_value = project(pair, 0)
    partial_rows = contract_rows(left_side, lax.all_gather(right_side, ROW, axis=1, tiled=True))
    mixed_sum = sum_at_owner(partial_rows, "col", 2)
    stream = finish(pair, mixed_sum, gate_value, 0)
    left_side, right_side, gate_value = project(stream, 1)
    left_rows = gather_directly(left_side, "col", 2)
    column_strip = two_step_exchange(left_rows, ("row_0", "row_1"), (1, 0), 2, 1)
    mixed_sum = contract_columns(column_strip, lax.all_gather(right_side, ROW, axis=1, tiled=True))
    stream = finish(stream, mixed_sum, gate_value, 1)
    normed = layer_norm(stream.astype(jnp.float32), 2).astype(jnp.bfloat16)
    inner_sum = jnp.dot(normed, trans_in, preferred_element_type=jnp.float32)
    activation = (jax.nn.silu(inner_sum[..., :ffn_width]) * inner_sum[..., ffn_width:]).astype(
        jnp.bfloat16
    )
    update = jnp.dot(activation, trans_out, preferred_element_type=jnp.float32)
    return (stream.astype(jnp.float32) + keep_mask[:, :, None] * update).astype(jnp.bfloat16)


def solution(mesh):
    torus = Mesh(
        mesh.devices.reshape(mesh.shape["grp"], 16, 2, mesh.shape["col"]),
        ("grp", "row_0", "row_1", "col"),
    )
    placed = (P(GRP_ROW, "col", None), P("grp"), P(), P(), P(), P(), P())
    return jax.shard_map(
        body, mesh=torus, in_specs=placed, out_specs=P(GRP_ROW, "col", None), check_vma=False
    )
```

profile of v0, /device:TPU:33, one launch (start us, length us, event | category | flops | bytes accessed | tf_op | source)
XLA Modules:
  0.0 327.6 jit_solution(5073324090975161739)
XLA Ops:
  7.2 1.1 convert_reduce_fusion
  8.4 1.4 fusion.20
  9.9 1.0 fusion.74
  10.9 0.1 copy.77
  11.0 0.1 broadcast_multiply_fusion.5
  11.1 1.5 convolution_bitcast_fusion.1
  12.6 1.1 fusion.37
  13.7 0.1 all-gather.3.cloned.1.call-update
  13.7 1.2 copy.55
  14.9 91.9 %all-gather.3.cloned.1.call-done = bf16[128,384,96]{0,2,1:T(8,128)(2,1)} async-done(((bf16[128,12,96]{0,2,1:T(8,128)(2,1)}), bf16[128,384,96]{0,2,1:T(8,128)(2,1)}) %all-gather.3.cloned.1.call-update) | async-done | bytes 9437200 | tf_op jit(solution)/shard_map/all_gather | solution.py:104
  106.8 15.6 %copy.56 = bf16[128,384,96]{2,1,0:T(8,128)(2,1)} copy(bf16[128,384,96]{0,2,1:T(8,128)(2,1)} %all-gather.3.cloned.1.call-done) | data formatting | bytes 18874368 | tf_op jit(solution)/shard_map/all_gather | solution.py:104
  122.4 9.2 %fusion.78 = f32[128,12,384]{2,1,0:T(8,128)S(1)} fusion(bf16[128,12,96]{2,1,0:T(8,128)(2,1)} %copy.55, bf16[128,384,96]{2,1,0:T(8,128)(2,1)} %copy.56), kind=kOutput, calls=%fused_computation.114 | convolution fusion | flops 113246208 | bytes 12091392 | tf_op jit(solution)/shard_map/hik,hjk->hij/dot_general | solution.py:61
  131.6 2.1 copy.57
  133.7 3.3 copy.58
  136.9 4.1 %all-to-all-start = ((f32[4,128,12,96]{1,3,2,0:T(8,128)}), f32[4,128,12,96]{1,3,2,0:T(8,128)S(1)}, u32[]{:S(2)}, u32[]{:S(2)}) async-start(f32[4,128,12,96]{1,3,2,0:T(8,128)} %copy.58), calls=%async_computation | async-start | bytes 4718592 | tf_op jit(solution)/shard_map/all_to_all | solution.py:19
  141.1 0.8 copy.81
  141.8 1.3 fusion.11
  143.1 26.6 %all-to-all-done = f32[4,128,12,96]{1,3,2,0:T(8,128)S(1)} async-done(((f32[4,128,12,96]{1,3,2,0:T(8,128)}), f32[4,128,12,96]{1,3,2,0:T(8,128)S(1)}, u32[]{:S(2)}, u32[]{:S(2)}) %all-to-all-start) | async-done | bytes 2359328 | tf_op jit(solution)/shard_map/all_to_all | solution.py:19
  169.7 0.3 fusion.73
  170.1 0.5 multiply_reduce_fusion.3
  170.6 0.8 fusion.75
  171.3 0.5 multiply_reduce_fusion.2
  171.8 0.5 convolution_bitcast_fusion
  172.4 1.1 fusion.23
  173.5 0.2 broadcast_in_dim.2
  173.7 17.4 %all_to_all.20 = bf16[4,128,12,96]{1,3,2,0:T(8,128)(2,1)S(1)} all-to-all(bf16[4,128,12,96]{1,3,2,0:T(8,128)(2,1)S(1)} %broadcast_in_dim.2), channel_id=1, replica_groups=mesh['grp'=2,'row_0'=16,'row_1'=2,'col'=4] {'col'}, dimensions={0} | all-to-all | bytes 2359296 | tf_op jit(solution)/shard_map/all_to_all | solution.py:25
  191.0 1.1 copy.62
  192.1 2.2 reshape_reshape.3
  194.3 0.5 copy.63
  194.8 7.1 %all_to_all.21 = bf16[16,2,128,12,12]{2,0,4,3,1:T(8,128)(2,1)S(1)} all-to-all(bf16[16,2,128,12,12]{2,0,4,3,1:T(8,128)(2,1)S(1)} %copy.63), channel_id=1, replica_groups=mesh['grp'=2,'row_0'=16,'row_1'=2,'col'=4] {'row_1'}, dimensions={1} | all-to-all | bytes 2359296 | tf_op jit(solution)/shard_map/all_to_all | solution.py:43
  201.9 2.2 copy.64
  204.1 6.6 %all-to-all-start.3 = ((bf16[16,2,128,12,12]{2,1,4,3,0:T(2,128)(2,1)}), bf16[16,2,128,12,12]{2,1,4,3,0:T(2,128)(2,1)S(1)}, u32[]{:S(2)}, u32[]{:S(2)}) async-start(bf16[16,2,128,12,12]{2,1,4,3,0:T(2,128)(2,1)} %copy.64), calls=%async_computation.3 | async-start | bytes 2359296 | tf_op jit(solution)/shard_map/all_to_all | solution.py:43
  210.7 0.5 fusion.8
  211.2 66.2 %all-to-all-done.3 = bf16[16,2,128,12,12]{2,1,4,3,0:T(2,128)(2,1)S(1)} async-done(((bf16[16,2,128,12,12]{2,1,4,3,0:T(2,128)(2,1)}), bf16[16,2,128,12,12]{2,1,4,3,0:T(2,128)(2,1)S(1)}, u32[]{:S(2)}, u32[]{:S(2)}) %all-to-all-start.3) | async-done | bytes 1179680 | tf_op jit(solution)/shard_map/all_to_all | solution.py:43
  277.4 1.0 copy.65
  278.5 0.8 copy.66
  279.3 1.2 reshape.165
  280.4 2.2 copy.67
  282.6 12.4 %all-gather.5.cloned.1.call-done = bf16[128,384,96]{0,2,1:T(8,128)(2,1)} async-done(((bf16[128,12,96]{0,2,1:T(8,128)(2,1)}), bf16[128,384,96]{0,2,1:T(8,128)(2,1)}) %all-gather.5.cloned.1.call-update) | async-done | bytes 9437200 | tf_op jit(solution)/shard_map/all_gather | solution.py:110
  295.0 15.6 %copy.68 = bf16[128,384,96]{2,1,0:T(8,128)(2,1)} copy(bf16[128,384,96]{0,2,1:T(8,128)(2,1)} %all-gather.5.cloned.1.call-done) | data formatting | bytes 18874368 | tf_op jit(solution)/shard_map/all_gather | solution.py:110
  310.6 5.8 %fusion.76 = (f32[12,96]{1,0:T(8,128)S(1)}, f32[128,12,96]{2,1,0:T(8,128)S(1)}) fusion(bf16[128,384,12]{1,2,0:T(8,128)(2,1)S(1)} %copy.67, bf16[128,384,96]{2,1,0:T(8,128)(2,1)} %copy.68), kind=kOutput, calls=%fused_computation.112 | convolution fusion | flops 113392512 | bytes 11211264 | tf_op jit(solution)/shard_map/hki,hkj->hij/dot_general | solution.py:65
  316.4 0.2 multiply_reduce_fusion
  316.6 0.1 multiply_convert_fusion
  316.8 0.5 copy-done.4
  317.2 0.6 fusion.77
  317.9 0.5 multiply_reduce_fusion.1
  318.4 0.8 fusion.53
  319.3 1.5 fusion.16
  (30 shorter events, 0.3 us)
Async XLA Ops:
  6.5 311.8 %copy-start = (bf16[128,1024]{1,0:T(8,128)(2,1)S(1)}, bf16[128,1024]{1,0:T(8,128)(2,1)}, u32[]{:S(2)}) copy-start(bf16[128,1024]{1,0:T(8,128)(2,1)} %param.12) | copy-start | bytes 786436
  6.6 100.3 %all-gather.3.cloned.1.call-start = ((), (), s32[]{:S(2)}) async-start(), calls=%async_computation.4 | async-start | bytes 9732096 | tf_op jit(solution)/shard_map/all_gather | solution.py:104
  9.9 1.2 copy-start.5
  136.9 4.9 %copy-start.1 = (bf16[12,96,128]{2,1,0:T(8,128)(2,1)S(1)}, bf16[12,96,128]{2,1,0:T(8,128)(2,1)}, u32[]{:S(2)}) copy-start(bf16[12,96,128]{2,1,0:T(8,128)(2,1)} %param.7) | copy-start | bytes 884740
  136.9 32.8 %all-to-all-start = ((f32[4,128,12,96]{1,3,2,0:T(8,128)}), f32[4,128,12,96]{1,3,2,0:T(8,128)S(1)}, u32[]{:S(2)}, u32[]{:S(2)}) async-start(f32[4,128,12,96]{1,3,2,0:T(8,128)} %copy.58), calls=%async_computation | async-start | bytes 4718592 | tf_op jit(solution)/shard_map/all_to_all | solution.py:19
  141.1 153.9 %all-gather.5.cloned.1.call-start = ((), (), s32[]{:S(2)}) async-start(), calls=%async_computation.5 | async-start | bytes 9732096 | tf_op jit(solution)/shard_map/all_gather | solution.py:110
  169.7 0.8 copy-start.3
  170.0 1.8 copy-start.2
  201.9 8.8 %copy-start.7 = (bf16[2,128,128]{2,1,0:T(8,128)(2,1)S(1)}, bf16[2,128,128]{2,1,0:T(8,128)(2,1)}, u32[]{:S(2)}) copy-start(bf16[2,128,128]{2,1,0:T(8,128)(2,1)} %param.10) | copy-start | bytes 196612
  204.1 73.3 %all-to-all-start.3 = ((bf16[16,2,128,12,12]{2,1,4,3,0:T(2,128)(2,1)}), bf16[16,2,128,12,12]{2,1,4,3,0:T(2,128)(2,1)S(1)}, u32[]{:S(2)}, u32[]{:S(2)}) async-start(bf16[16,2,128,12,12]{2,1,4,3,0:T(2,128)(2,1)} %copy.64), calls=%async_computation.3 | async-start | bytes 2359296 | tf_op jit(solution)/shard_map/all_to_all | solution.py:43
  316.4 0.8 copy-start.4
  318.4 0.9 copy-start.6
Sparse Core Ops, SparseCore 0:
  13.8 92.9 all-gather.2
  173.6 121.3 all-gather.4
where the time goes:
time: 329 us; the launch traced here: 328 us
  waiting for transfers between devices  197 us (60%)
  local copies, waits for them, and re-layouts  51.5 us (16%)
  blocking collectives  24.4 us (7%)
  matrix products  22.5 us (7%)
  between operations  14.4 us (4%)
  starting transfers between devices  10.7 us (3%)
  other arithmetic  6.82 us (2%)
    all_gather x2, waiting for transfers between devices, body(): lax.all_gather(right_side, ROW, axis=1, tiled=True)  104 us
    all_to_all x1, waiting for transfers between devices, exchange_in_order(): lax.all_to_all(blocks, axes[k], split_axis=k, concat_axis=k, tiled=True)  66.2 us
    all_gather x2, local copies, waits for them, and re-layouts, body(): lax.all_gather(right_side, ROW, axis=1, tiled=True)  31.1 us
    all_to_all x1, waiting for transfers between devices, sum_at_owner(): lax.all_to_all(blocks, axis, split_axis=0, concat_axis=0, tiled=True)  26.6 us
    all_to_all x1, blocking collectives, sent_to_all(): return lax.all_to_all(copies, axis, split_axis=0, concat_axis=0, tiled=True)  17.4 us
    dot_general x1, matrix products, contract_rows(): jnp.einsum('hik,hjk->hij', left_side, right_side, preferred_element_type=...  9.19 us
    all_to_all x1, blocking collectives, exchange_in_order(): lax.all_to_all(blocks, axes[k], split_axis=k, concat_axis=k, tiled=True)  7.07 us
    all_to_all x1, starting transfers between devices, exchange_in_order(): lax.all_to_all(blocks, axes[k], split_axis=k, concat_axis=k, tiled=True)  6.6 us
  transfers between devices with their start and end apart: 4, of which 4 were waited for; matrix products, arithmetic and copies ran while one was open for 5% of the time, Pallas kernels for 0%

commit v1 on v0

v1 whole, which is shorter than its diff:
```python
import jax
import jax.numpy as jnp
from jax import lax
from jax.sharding import Mesh
from jax.sharding import PartitionSpec as P

ROW = ("row_0", "row_1")
GRP_ROW = ("grp", "row_0", "row_1")
NAMES = ("row_0", "row_1", "col")


def layer_norm(values, along):
    average = jnp.mean(values, axis=along, keepdims=True)
    centred = values - average
    spread = jnp.mean(centred * centred, axis=along, keepdims=True)
    return centred * lax.rsqrt(spread + 1e-05)


def exchange(blocks):
    return lax.all_to_all(blocks, NAMES, split_axis=0, concat_axis=0, tiled=True)


def body(pair, token_count, tri_in, tri_gate, tri_out, trans_in, trans_out):
    tile_rows, tile_cols, pair_width = pair.shape
    hidden = tri_out.shape[1]
    ffn_width = trans_out.shape[0]
    n_row = lax.axis_size("row_0") * lax.axis_size("row_1")
    n_col = lax.axis_size("col")
    row_place = lax.axis_index(ROW)
    col_place = lax.axis_index("col")
    token_limit = token_count[0]
    row_keep = (row_place * tile_rows + jnp.arange(tile_rows, dtype=jnp.int32) < token_limit).astype(jnp.float32)
    col_keep = (col_place * tile_cols + jnp.arange(tile_cols, dtype=jnp.int32) < token_limit).astype(jnp.float32)
    keep_mask = row_keep[:, None] * col_keep[None, :]
    tokens = n_row * tile_rows

    def triangle(stream, side):
        normed = layer_norm(stream.astype(jnp.float32), 2).astype(jnp.bfloat16)
        weight = tri_in[side].reshape(pair_width, 4, hidden)
        projected = jnp.einsum("ijc,cgh->ghij", normed, weight, preferred_element_type=jnp.float32)
        both = (keep_mask * jax.nn.sigmoid(projected[2:]) * projected[:2]).astype(jnp.bfloat16)
        gate_value = jax.nn.sigmoid(jnp.dot(normed, tri_gate[side], preferred_element_type=jnp.float32))
        got = exchange(both.transpose(1, 0, 2, 3))
        got = got.reshape(n_row, n_col, 2, tile_rows, tile_cols).transpose(2, 0, 3, 1, 4).reshape(2, tokens, tokens)
        if side == 0:
            mixed = lax.dot_general(got[0], got[1], (((1,), (1,)), ((), ())), preferred_element_type=jnp.float32)
        else:
            mixed = lax.dot_general(got[0], got[1], (((0,), (0,)), ((), ())), preferred_element_type=jnp.float32)
        mixed = mixed.astype(jnp.bfloat16).reshape(n_row, tile_rows, n_col, tile_cols).transpose(0, 2, 1, 3)
        back = exchange(mixed.reshape(n_row * n_col, tile_rows, tile_cols))
        mixnorm = layer_norm(back.astype(jnp.float32), 0).astype(jnp.bfloat16)
        update = gate_value * jnp.einsum("hij,hc->ijc", mixnorm, tri_out[side], preferred_element_type=jnp.float32)
        return (stream.astype(jnp.float32) + keep_mask[:, :, None] * update).astype(jnp.bfloat16)

    stream = triangle(pair, 0)
    stream = triangle(stream, 1)
    normed = layer_norm(stream.astype(jnp.float32), 2).astype(jnp.bfloat16)
    inner_sum = jnp.dot(normed, trans_in, preferred_element_type=jnp.float32)
    activation = (jax.nn.silu(inner_sum[..., :ffn_width]) * inner_sum[..., ffn_width:]).astype(jnp.bfloat16)
    update = jnp.dot(activation, trans_out, preferred_element_type=jnp.float32)
    return (stream.astype(jnp.float32) + keep_mask[:, :, None] * update).astype(jnp.bfloat16)


def solution(mesh):
    cores = 2
    torus = Mesh(
        mesh.devices.reshape(mesh.shape["grp"], mesh.shape["row"] // cores, cores, mesh.shape["col"]),
        ("grp", "row_0", "row_1", "col"),
    )
    placed = (P(GRP_ROW, "col", None), P("grp"), P(), P(), P(), P(), P())
    return jax.shard_map(body, mesh=torus, in_specs=placed, out_specs=P(GRP_ROW, "col", None), check_vma=False)
```

time: 329 us -> 228 us (0.69)
  waiting for transfers between devices: 197 us -> 63.7 us
  blocking collectives: 24.4 us -> 125 us
  local copies, waits for them, and re-layouts: 51.5 us -> 8.4 us
  matrix products: 22.5 us -> 6.4 us
  between operations: 14.4 us -> 1.09 us
  starting transfers between devices: 10.7 us -> 16.9 us
    all_gather x2 -> x0, waiting for transfers between devices: 104 us -> none  [body(): lax.all_gather(right_side, ROW, axis=1, tiled=True)]
    all_to_all x2, blocking collectives: 24.4 us -> 125 us  [exchange(): lax.all_to_all(blocks, NAMES, split_axis=0, concat_axis=0, tiled=True)]
    all_gather x2 -> x0, local copies, waits for them, and re-layouts: 31.1 us -> none  [body(): lax.all_gather(right_side, ROW, axis=1, tiled=True)]
    all_to_all x2, waiting for transfers between devices: 92.9 us -> 63.7 us  [exchange(): lax.all_to_all(blocks, NAMES, split_axis=0, concat_axis=0, tiled=True)]
    dot_general x8, matrix products: 20.2 us -> 4.07 us  [the longest x2 1.28 us: triangle(): jnp.einsum('hij,hc->ijc', mixnorm, tri_out[side], preferred_element_type=...]
    all_to_all x2, starting transfers between devices: 10.7 us -> 16.9 us  [exchange(): lax.all_to_all(blocks, NAMES, split_axis=0, concat_axis=0, tiled=True)]
    transpose x3 -> x2, local copies, waits for them, and re-layouts: 5.19 us -> 1.45 us  [triangle(): got = exchange(both.transpose(1, 0, 2, 3))]
  transfers between devices with their start and end apart: 4 -> 2, of which waited for: 4 -> 2; matrix products, arithmetic and copies ran while one was open for 5% -> 0% of each run, Pallas kernels for 0% -> 0%
where the time goes in v1:
time: 228 us; the launch traced here: 227 us
  blocking collectives  125 us (55%)
  waiting for transfers between devices  63.7 us (28%)
  starting transfers between devices  16.9 us (7%)
  local copies, waits for them, and re-layouts  8.4 us (4%)
  matrix products  6.4 us (3%)
  other arithmetic  5.39 us (2%)
    all_to_all x2, blocking collectives, exchange(): lax.all_to_all(blocks, NAMES, split_axis=0, concat_axis=0, tiled=True)  125 us
    all_to_all x2, waiting for transfers between devices, exchange(): lax.all_to_all(blocks, NAMES, split_axis=0, concat_axis=0, tiled=True)  63.7 us
    all_to_all x2, starting transfers between devices, exchange(): lax.all_to_all(blocks, NAMES, split_axis=0, concat_axis=0, tiled=True)  16.9 us
  transfers between devices with their start and end apart: 2, of which 2 were waited for; matrix products, arithmetic and copies ran while one was open for 0% of the time, Pallas kernels for 0%

profile of v1, /device:TPU:33, one launch (start us, length us, event | category | flops | bytes accessed | tf_op | source)
XLA Modules:
  0.0 227.3 jit_solution(3984759160672727945)
XLA Ops:
  0.7 1.1 convert_reduce_fusion.2
  1.9 1.4 fusion.38
  3.3 1.0 fusion.64
  4.6 0.5 convolution_bitcast_fusion.1
  5.1 0.4 fusion.40
  5.4 0.7 copy.26
  6.2 74.1 %all_to_all.20 = bf16[128,2,12,96]{3,1,2,0:T(2,128)(2,1)S(1)} all-to-all(bf16[128,2,12,96]{3,1,2,0:T(2,128)(2,1)S(1)} %copy.26), channel_id=1, replica_groups=mesh['grp'=2,'row_0'=16,'row_1'=2,'col'=4] {'row_0','row_1','col'}, dimensions={0} | all-to-all | bytes 1179648 | tf_op jit(solution)/shard_map/all_to_all | solution.py:20
  80.3 0.2 copy.27
  80.5 0.4 fusion.63
  80.8 0.1 copy.29
  81.0 0.3 squeeze.30
  81.3 0.1 copy.28
  81.4 0.3 squeeze.29
  81.7 0.3 convolution_convert_fusion.1
  82.0 0.3 reshape.155
  82.3 0.2 copy.30
  82.5 1.1 copy.31
  83.5 8.5 %all-to-all-start.1 = ((bf16[128,12,96]{2,1,0:T(8,128)(2,1)}), bf16[128,12,96]{2,1,0:T(8,128)(2,1)S(1)}, u32[]{:S(2)}, u32[]{:S(2)}) async-start(bf16[128,12,96]{2,1,0:T(8,128)(2,1)} %copy.31), calls=%async_computation.1 | async-start | bytes 1048576 | tf_op jit(solution)/shard_map/all_to_all | solution.py:20
  92.1 0.5 fusion.11
  92.7 31.8 %all-to-all-done.1 = bf16[128,12,96]{2,1,0:T(8,128)(2,1)S(1)} async-done(((bf16[128,12,96]{2,1,0:T(8,128)(2,1)}), bf16[128,12,96]{2,1,0:T(8,128)(2,1)S(1)}, u32[]{:S(2)}, u32[]{:S(2)}) %all-to-all-start.1) | async-done | bytes 294944 | tf_op jit(solution)/shard_map/all_to_all | solution.py:20
  124.4 0.2 convert_reduce_fusion.1
  124.6 0.2 fusion.34
  124.8 0.1 fusion.35
  125.0 0.6 fusion.65
  125.6 0.5 multiply_reduce_fusion.1
  126.1 0.5 convolution_bitcast_fusion
  126.6 0.4 fusion.41
  127.0 0.7 copy.35
  127.7 51.3 %all_to_all.21 = bf16[128,2,12,96]{3,1,2,0:T(2,128)(2,1)S(1)} all-to-all(bf16[128,2,12,96]{3,1,2,0:T(2,128)(2,1)S(1)} %copy.35), channel_id=1, replica_groups=mesh['grp'=2,'row_0'=16,'row_1'=2,'col'=4] {'row_0','row_1','col'}, dimensions={0} | all-to-all | bytes 1179648 | tf_op jit(solution)/shard_map/all_to_all | solution.py:20
  179.0 0.2 copy.36
  179.2 0.4 fusion.62
  179.7 0.3 squeeze.34
  180.0 0.1 copy.37
  180.1 0.3 squeeze.33
  180.4 0.4 convolution_convert_fusion
  180.8 0.3 reshape.158
  181.0 0.2 copy.39
  181.2 1.1 copy.40
  182.3 8.5 %all-to-all-start.3 = ((bf16[128,12,96]{2,1,0:T(8,128)(2,1)}), bf16[128,12,96]{2,1,0:T(8,128)(2,1)S(1)}, u32[]{:S(2)}, u32[]{:S(2)}) async-start(bf16[128,12,96]{2,1,0:T(8,128)(2,1)} %copy.40), calls=%async_computation.3 | async-start | bytes 1048576 | tf_op jit(solution)/shard_map/all_to_all | solution.py:20
  190.7 0.5 fusion.8
  191.3 31.9 %all-to-all-done.3 = bf16[128,12,96]{2,1,0:T(8,128)(2,1)S(1)} async-done(((bf16[128,12,96]{2,1,0:T(8,128)(2,1)}), bf16[128,12,96]{2,1,0:T(8,128)(2,1)S(1)}, u32[]{:S(2)}, u32[]{:S(2)}) %all-to-all-start.3) | async-done | bytes 294944 | tf_op jit(solution)/shard_map/all_to_all | solution.py:20
  223.2 0.2 convert_reduce_fusion
  223.3 0.2 fusion.32
  223.6 0.1 fusion.33
  223.7 0.6 fusion.66
  224.4 0.5 multiply_reduce_fusion
  224.9 0.8 fusion.44
  225.8 1.5 fusion.20
  (26 shorter events, 0.6 us)
Async XLA Ops:
  0.0 224.8 %copy-start = (bf16[128,1024]{1,0:T(8,128)(2,1)S(1)}, bf16[128,1024]{1,0:T(8,128)(2,1)}, u32[]{:S(2)}) copy-start(bf16[128,1024]{1,0:T(8,128)(2,1)} %param.12) | copy-start | bytes 786436
  0.0 4.5 %copy-start.1 = (bf16[12,96,128]{2,1,0:T(8,128)(2,1)S(1)}, bf16[12,96,128]{2,1,0:T(8,128)(2,1)}, u32[]{:S(2)}) copy-start(bf16[12,96,128]{2,1,0:T(8,128)(2,1)} %param.7) | copy-start | bytes 884740
  82.5 9.7 %copy-start.4 = (bf16[2,128,128]{2,1,0:T(8,128)(2,1)S(1)}, bf16[2,128,128]{2,1,0:T(8,128)(2,1)}, u32[]{:S(2)}) copy-start(bf16[2,128,128]{2,1,0:T(8,128)(2,1)} %param.10) | copy-start | bytes 196612
  83.5 40.9 %all-to-all-start.1 = ((bf16[128,12,96]{2,1,0:T(8,128)(2,1)}), bf16[128,12,96]{2,1,0:T(8,128)(2,1)S(1)}, u32[]{:S(2)}, u32[]{:S(2)}) async-start(bf16[128,12,96]{2,1,0:T(8,128)(2,1)} %copy.31), calls=%async_computation.1 | async-start | bytes 1048576 | tf_op jit(solution)/shard_map/all_to_all | solution.py:20
  92.7 32.3 %copy-start.2 = (bf16[2,128,128]{2,1,0:T(8,128)(2,1)S(1)}, bf16[2,128,128]{2,1,0:T(8,128)(2,1)}, u32[]{:S(2)}) copy-start(bf16[2,128,128]{2,1,0:T(8,128)(2,1)} %param.11) | copy-start | bytes 196612
  182.3 40.9 %all-to-all-start.3 = ((bf16[128,12,96]{2,1,0:T(8,128)(2,1)}), bf16[128,12,96]{2,1,0:T(8,128)(2,1)S(1)}, u32[]{:S(2)}, u32[]{:S(2)}) async-start(bf16[128,12,96]{2,1,0:T(8,128)(2,1)} %copy.40), calls=%async_computation.3 | async-start | bytes 1048576 | tf_op jit(solution)/shard_map/all_to_all | solution.py:20
  224.8 0.9 copy-start.3

commit v2 on v1

v2 whole, which is shorter than its diff:
```python
import functools

import jax
import jax.numpy as jnp
from jax import lax
from jax.experimental import pallas as pl
from jax.experimental.pallas import tpu as pltpu
from jax.sharding import Mesh
from jax.sharding import PartitionSpec as P

MESH = pl.DeviceIdType.MESH
F32, BF16 = jnp.float32, jnp.bfloat16
CORES = 2


def log2(n):
    assert n & (n - 1) == 0
    return n.bit_length() - 1


def dot(a, b, ca, cb):
    return lax.dot_general(a, b, (((ca,), (cb,)), ((), ())), preferred_element_type=F32)


def layer_norm(v):
    average = jnp.mean(v, axis=0, keepdims=True)
    centred = v - average
    spread = jnp.mean(centred * centred, axis=0, keepdims=True)
    return centred * lax.rsqrt(spread + 1e-05)


def one_hot(shape, source_of_row):
    row = lax.broadcasted_iota(jnp.int32, shape, 0)
    col = lax.broadcasted_iota(jnp.int32, shape, 1)
    return (source_of_row(row) == col).astype(F32).astype(BF16)


def kernel(
    dims, count_ref, pair_ref, tri_in_ref, tri_gate_ref, tri_out_ref, trans_in_ref, trans_out_ref, out_ref,
    stream, normed, gate, keep, z_out, z_in, x_out, x_in, left, right, mixed,
    xb_out, xb_in, zb_out, zb_in, zs, zr, xs, xr, zbs, zbr, xbs, xbr,
):
    nz, nx, ti, tk = dims
    nc = CORES
    np_ = nc * nx
    tile, chan = pair_ref.shape
    hidden = tri_out_ref.shape[1]
    ffn = trans_out_ref.shape[0]
    size = nx * tk
    z, c, x = lax.axis_index("row_0"), lax.axis_index("row_1"), lax.axis_index("col")
    me = c * nx + x
    step = tile // 3
    pieces = [slice(k * step, (k + 1) * step) for k in range(3)]
    far_first = sorted(range(1, nz), key=lambda d: -min(d, nz - d))

    def z_peer(d):
        return lax.rem(z + d, nz)

    others = [(dc, dx) for dx in sorted(range(nx), key=lambda d: -min(d, nx - d)) for dc in range(nc) if dc or dx]

    def x_peer(o):
        return lax.rem(c + o[0], nc), lax.rem(x + o[1], nx)

    barrier = pltpu.get_barrier_semaphore()
    for d in far_first:
        pl.semaphore_signal(barrier, inc=1, device_id={"row_0": z_peer(d)}, device_id_type=MESH)
    for o in others:
        tc, tx = x_peer(o)
        pl.semaphore_signal(barrier, inc=1, device_id={"row_1": tc, "col": tx}, device_id_type=MESH)

    def z_exchange(source, target, ss, rs):
        copies = []
        for n, d in enumerate(far_first):
            t = z_peer(d)
            copy = pltpu.make_async_remote_copy(
                src_ref=source.at[t], dst_ref=target.at[z], send_sem=ss.at[n], recv_sem=rs.at[n],
                device_id={"row_0": t}, device_id_type=MESH,
            )
            copy.start()
            copies.append(copy)
        target[z] = source[z]
        return copies

    def x_exchange(source, target, ss, rs):
        copies = []
        for n, o in enumerate(others):
            tc, tx = x_peer(o)
            copy = pltpu.make_async_remote_copy(
                src_ref=source.at[tc * nx + tx], dst_ref=target.at[me], send_sem=ss.at[n], recv_sem=rs.at[n],
                device_id={"row_1": tc, "col": tx}, device_id_type=MESH,
            )
            copy.start()
            copies.append(copy)
        target[me] = source[me]
        return copies

    def finish(copies):
        for copy in copies:
            copy.wait()

    token = lax.broadcasted_iota(jnp.int32, (1, tile), 1)
    row = sum((token >= k * tk).astype(jnp.int32) for k in range(1, ti))
    limit = count_ref[0]
    inside = ((z * nc + c) * ti + row < limit) & (x * tk + token - row * tk < limit)
    keep[...] = jnp.where(inside, 1.0, 0.0).astype(F32)

    for piece in pieces:
        stream[:, piece] = pair_ref[piece, :].astype(F32).T.astype(BF16)

    lz, lp = log2(nz), log2(np_)

    for side in range(2):
        w_in = tri_in_ref[side]
        for piece in pieces:
            v = layer_norm(stream[:, piece].astype(F32)).astype(BF16)
            normed[:, piece] = v
            value = dot(w_in, v, 0, 0)
            both = keep[:, piece] * jax.nn.sigmoid(value[2 * hidden :]) * value[: 2 * hidden]
            both = both.astype(BF16)
            for k in range(nz):
                z_out[side, k, 0:np_, piece] = both[k * np_ : (k + 1) * np_]
                z_out[side, k, np_ : 2 * np_, piece] = both[hidden + k * np_ : hidden + (k + 1) * np_]
        if side == 0:
            pl.semaphore_wait(barrier, len(far_first) + len(others))
        copies = z_exchange(z_out.at[side], z_in.at[side], zs.at[side], zr.at[side])
        for piece in pieces:
            gate[:, piece] = jax.nn.sigmoid(dot(tri_gate_ref[side], normed[:, piece], 0, 0))
        n = 2 * hidden
        swap = one_hot((n, n), lambda r: ((r & (2 * nz - 1)) & (nz - 1)) * (2 * np_) + ((r >> lz) & 1) * np_ + (r >> (lz + 1)))
        finish(copies)
        for piece in pieces:
            got = z_in[side, :, :, piece].reshape(n, step)
            x_out[side, :, :, piece] = dot(swap, got, 1, 0).astype(BF16).reshape(np_, 2 * nz, step)
        copies = x_exchange(x_out.at[side], x_in.at[side], xs.at[side], xr.at[side])
        order = one_hot((size, size), lambda r: (r & (nz - 1)) * (nc * ti) + (r >> lz))
        finish(copies)
        for cc in range(nc):
            for i in range(ti):
                rows = slice((cc * ti + i) * nz, (cc * ti + i + 1) * nz)
                for xx in range(nx):
                    cols = slice(xx * tk, (xx + 1) * tk)
                    left[rows, cols] = x_in[side, cc * nx + xx, 0:nz, i * tk : (i + 1) * tk]
                    right[rows, cols] = x_in[side, cc * nx + xx, nz : 2 * nz, i * tk : (i + 1) * tk]
        if side == 0:
            product = dot(left[...], right[...], 1, 1).astype(BF16)
            mixed[...] = dot(product, order, 1, 0).astype(BF16)
        else:
            turned = dot(order, left[...], 1, 1).astype(BF16)
            mixed[...] = dot(turned, right[...], 1, 0).astype(BF16)
        for cc in range(nc):
            for i in range(ti):
                rows = slice((cc * ti + i) * nz, (cc * ti + i + 1) * nz)
                for xx in range(nx):
                    xb_out[side, cc * nx + xx, :, i * tk : (i + 1) * tk] = mixed[rows, xx * tk : (xx + 1) * tk]
        copies = x_exchange(xb_out.at[side], xb_in.at[side], xbs.at[side], xbr.at[side])
        swap = one_hot((hidden, hidden), lambda r: (r & (np_ - 1)) * nz + (r >> lp))
        finish(copies)
        for piece in pieces:
            got = xb_in[side, :, :, piece].reshape(hidden, step)
            zb_out[side, :, :, piece] = dot(swap, got, 1, 0).astype(BF16).reshape(nz, np_, step)
        copies = z_exchange(zb_out.at[side], zb_in.at[side], zbs.at[side], zbr.at[side])
        finish(copies)
        for piece in pieces:
            got = zb_in[side, :, :, piece].reshape(hidden, step)
            v = layer_norm(got.astype(F32)).astype(BF16)
            update = gate[:, piece] * dot(tri_out_ref[side], v, 0, 0)
            stream[:, piece] = (stream[:, piece].astype(F32) + keep[:, piece] * update).astype(BF16)

    for piece in pieces:
        base = stream[:, piece].astype(F32)
        v = layer_norm(base).astype(BF16)
        inner = dot(trans_in_ref[...], v, 0, 0)
        act = (jax.nn.silu(inner[:ffn]) * inner[ffn:]).astype(BF16)
        update = dot(trans_out_ref[...], act, 0, 0)
        out_ref[piece, :] = (base + keep[:, piece] * update).T.astype(BF16)


def body(pair, token_count, tri_in, tri_gate, tri_out, trans_in, trans_out):
    ti, tk, chan = pair.shape
    hidden = tri_out.shape[1]
    nz, nx = lax.axis_size("row_0"), lax.axis_size("col")
    np_ = CORES * nx
    tile, size = ti * tk, nx * tk
    vmem = pl.BlockSpec(memory_space=pltpu.VMEM)
    sem = pltpu.SemaphoreType.DMA
    out = pl.pallas_call(
        functools.partial(kernel, (nz, nx, ti, tk)),
        out_shape=jax.ShapeDtypeStruct((tile, chan), BF16),
        in_specs=[pl.BlockSpec(memory_space=pltpu.SMEM)] + [vmem] * 6,
        out_specs=vmem,
        scratch_shapes=[
            pltpu.VMEM((chan, tile), BF16),
            pltpu.VMEM((chan, tile), BF16),
            pltpu.VMEM((chan, tile), F32),
            pltpu.VMEM((1, tile), F32),
            pltpu.VMEM((2, nz, 2 * np_, tile), BF16),
            pltpu.VMEM((2, nz, 2 * np_, tile), BF16),
            pltpu.VMEM((2, np_, 2 * nz, tile), BF16),
            pltpu.VMEM((2, np_, 2 * nz, tile), BF16),
            pltpu.VMEM((size, size), BF16),
            pltpu.VMEM((size, size), BF16),
            pltpu.VMEM((size, size), BF16),
            pltpu.VMEM((2, np_, nz, tile), BF16),
            pltpu.VMEM((2, np_, nz, tile), BF16),
            pltpu.VMEM((2, nz, np_, tile), BF16),
            pltpu.VMEM((2, nz, np_, tile), BF16),
            sem((2, nz)), sem((2, nz)), sem((2, np_)), sem((2, np_)),
            sem((2, nz)), sem((2, nz)), sem((2, np_)), sem((2, np_)),
        ],
        compiler_params=pltpu.CompilerParams(
            collective_id=0, has_side_effects=True, vmem_limit_bytes=56 * 1024 * 1024
        ),
        name="pairformer_block",
    )(token_count, pair.reshape(tile, chan), tri_in, tri_gate, tri_out, trans_in, trans_out)
    return out.reshape(ti, tk, chan)


def solution(mesh):
    torus = Mesh(
        mesh.devices.reshape(mesh.shape["grp"], mesh.shape["row"] // CORES, CORES, mesh.shape["col"]),
        ("grp", "row_0", "row_1", "col"),
    )
    grp_row = ("grp", "row_0", "row_1")
    placed = (P(grp_row, "col", None), P("grp"), P(), P(), P(), P(), P())
    return jax.shard_map(
        body, mesh=torus, in_specs=placed, out_specs=P(grp_row, "col", None), check_vma=False
    )
```

time: 228 us -> 151 us (0.66)
  Pallas kernels: 0 us -> 147 us
  blocking collectives: 125 us -> 0 us
  waiting for transfers between devices: 63.7 us -> 0 us
  starting transfers between devices: 16.9 us -> 0 us
  local copies, waits for them, and re-layouts: 8.4 us -> 1.69 us
  matrix products: 6.4 us -> 0 us
  other arithmetic: 5.39 us -> 0 us
    pallas_call x0 -> x1, Pallas kernels: none -> 147 us  [body(): pl.pallas_call(functools.partial(kernel, (nz, nx, ti, tk)), out_shape=jax...]
    all_to_all x2 -> x0, blocking collectives: 125 us -> none  [exchange(): lax.all_to_all(blocks, NAMES, split_axis=0, concat_axis=0, tiled=True)]
    all_to_all x2 -> x0, waiting for transfers between devices: 63.7 us -> none  [exchange(): lax.all_to_all(blocks, NAMES, split_axis=0, concat_axis=0, tiled=True)]
    all_to_all x2 -> x0, starting transfers between devices: 16.9 us -> none  [exchange(): lax.all_to_all(blocks, NAMES, split_axis=0, concat_axis=0, tiled=True)]
    dot_general x10 -> x0, matrix products: 6.4 us -> none  [the longest x1 1.5 us: body(): update = jnp.dot(activation, trans_out, preferred_element_type=jnp.float32)]
    reduce_sum x8 -> x0, other arithmetic: 4.24 us -> none  [the longest x5 2.78 us: layer_norm(): spread = jnp.mean(centred * centred, axis=along, keepdims=True)]
    reshape x6 -> x0, local copies, waits for them, and re-layouts: 2.95 us -> none  [the longest x2 2.12 us: triangle(): back = exchange(mixed.reshape(n_row * n_col, tile_rows, tile_cols))]
    slice x7 -> x0, local copies, waits for them, and re-layouts: 2.29 us -> none  [the longest x4 1.03 us: triangle(): got[1]]
  transfers between devices with their start and end apart: 2 -> 0, of which waited for: 2 -> 0; matrix products, arithmetic and copies ran while one was open for 0% -> 0% of each run, Pallas kernels for 0% -> 0%
where the time goes in v2:
time: 151 us; the launch traced here: 149 us
  Pallas kernels  147 us (97%)
  local copies, waits for them, and re-layouts  1.69 us (1%)
    pallas_call x1, Pallas kernels, body(): pl.pallas_call(functools.partial(kernel, (nz, nx, ti, tk)), out_shape=jax...  147 us

profile of v2, /device:TPU:33, one launch (start us, length us, event | category | flops | bytes accessed | tf_op | source)
XLA Modules:
  0.0 149.3 jit_solution(3101354565702506274)
XLA Ops:
  0.7 146.9 %pairformer_block.1 = bf16[1152,128]{1,0:T(8,128)(2,1)} custom-call(s32[1]{0:T(128)S(6)} %copy.9.count_ref, bf16[1152,128]{1,0:T(8,128)(2,1)} %bitcast.3, bf16[2,128,512]{2,1,0:T(8,128)(2,1)} %tri_in_ref.1, bf16[2,128,128]{2,1,0:T(8,128)(2,1)} %tri_gate_ref.1, bf16[2,128,128]{2,1,0:T(8,128)(2,1)} %tri_out_ref.1, bf16[128,1024]{1,0:T(8,128)(2,1)} %trans_in_ref.1, ...), custom_call_target="tpu_custom_call" | custom-call | tf_op jit(solution)/shard_map/pairformer_block/pallas_call | solution.py:186
  147.6 1.7 %copy.10 = bf16[12,96,128]{2,1,0:T(8,128)(2,1)} copy(bf16[12,96,128]{2,1,0:T(8,128)(2,1)} %bitcast.2) | data formatting | bytes 589824
